TPU v7x, 32 devices: a whole 2x2x4 slice. The times are simulated.
32 devices in a mesh: groups: 2 (over x), row: 16 (over z, y, core).
Axes of the slice: x: 2, y: 2, z: 4, core: 2. Of those that a mesh axis runs over, the one named last changes fastest.
Arguments:
- latent: bfloat16 [8, 16, 128, 16], P('groups', None, 'row'), parts along dimension 0, may hold values from -16 to 16, as said below
- w_in: bfloat16 [3, 3, 3, 16, 384], replicated, may hold values from -0.3125 to 0.3125
- gain_one: float32 [384], replicated, may hold values from 0.25 to 1.75
- w_mid: bfloat16 [3, 3, 3, 384, 384], replicated, may hold values from -0.0625 to 0.0625
- gain_two: float32 [384], replicated, may hold values from 0.25 to 1.75
- w_up: bfloat16 [3, 3, 384, 192], replicated, may hold values from -0.109375 to 0.109375
- gain_three: float32 [192], replicated, may hold values from 0.25 to 1.75
- w_low: bfloat16 [3, 3, 3, 192, 96], replicated, may hold values from -0.078125 to 0.078125
- gain_four: float32 [96], replicated, may hold values from 0.25 to 1.75
- w_out: bfloat16 [3, 3, 3, 96, 3], replicated, may hold values from -0.125 to 0.125
Outputs:
- frames_rgb: float32 [8, 3, 32, 256], P('groups', None, 'row'), parts along dimension 0
There are 2 independent parts, one for each index of `groups`. A program takes and returns all parts, laid end to end along the dimension named above; an argument that names none is the same for every part. Nothing has to cross between parts.
Inputs may be any that keep to these rules, and one draw needn't show every extreme that they name: latent is real-valued.
All inputs are finite; a program needn't handle non-finite values.
Results may differ from a plain program's by a relative error of at most 0.0058.
Values may be sent and summed in bfloat16 or wider, within the bound.
A program may use at most 128 MiB of HBM per device.

v0:
```python
import functools

import jax
import jax.numpy as jnp
from jax import lax
from jax.experimental import pallas as pl
from jax.experimental.pallas import tpu as pltpu
from jax.sharding import PartitionSpec as P

eps = 1e-06
f32, bf16 = jnp.float32, jnp.bfloat16


def silu(z):
    return z / (1.0 + jnp.exp(-z))


def rms_act(field, gain):
    mean = jnp.mean(field * field, axis=-1, keepdims=True)
    return silu(field * lax.rsqrt(mean + eps) * gain)


def pair_norm(field, gain, low):
    half = field.shape[-1] // 2
    square = field * field
    first = jnp.sum(jnp.where(low, square, 0.0), axis=-1, keepdims=True)
    second = jnp.sum(jnp.where(low, 0.0, square), axis=-1, keepdims=True)
    scale = jnp.where(low, lax.rsqrt(first / half + eps), lax.rsqrt(second / half + eps))
    return silu(field * scale * gain)


def dot(a, b):
    return jnp.dot(a, b, preferred_element_type=f32)


def dot_t(a, b):
    return lax.dot_general(a, b, (((1,), (1,)), ((), ())), preferred_element_type=f32)


def kernel(
    sizes, devices,
    g_ref, gains_ref,
    win_hbm, wmid_hbm, wup_hbm, wlow_hbm, wout_ref,
    out_ref,
    raw_in, raw_up, raw_low,
    win, wmid, wup, wlow,
    gs, a1, first_mid, b0, b1, sent, a3, a3s, ys, part, got,
    wsem, send_sem, recv_sem, psend, precv,
):
    frames, cols, c0, c1, c2, c3, tall = sizes
    g1, g2 = gains_ref[0:1, 0:c1], gains_ref[1:2, 0:c1]
    g3, g4 = gains_ref[2:3, 0 : 2 * c2], gains_ref[3:4, 0 : wlow.shape[-1] // 2]
    me = lax.axis_index("row")
    is_first, is_last = me == 0, me == devices - 1
    has_up, has_down = me > 0, me < devices - 1

    copies = [pltpu.make_async_copy(win_hbm, raw_in, wsem.at[0])]
    copies.append(pltpu.make_async_copy(wup_hbm, raw_up, wsem.at[4]))
    copies.append(pltpu.make_async_copy(wlow_hbm, raw_low, wsem.at[5]))
    for i, a in enumerate((2, 1, 0)):
        copies.append(pltpu.make_async_copy(wmid_hbm.at[a], wmid.at[a], wsem.at[1 + i]))
    for copy in copies:
        copy.start()

    barrier = pltpu.get_barrier_semaphore()

    @pl.when(has_up)
    def _():
        pl.semaphore_signal(barrier, inc=1, device_id={"row": me - 1}, device_id_type=pl.DeviceIdType.MESH)

    @pl.when(has_down)
    def _():
        pl.semaphore_signal(barrier, inc=1, device_id={"row": me + 1}, device_id_type=pl.DeviceIdType.MESH)

    pl.semaphore_wait(barrier, has_up.astype(jnp.int32) + has_down.astype(jnp.int32))

    for t in range(frames):
        b1[t, cols:tall, :] = jnp.zeros((tall - cols, 3 * c1), bf16)

    @pl.when(is_first)
    def _():
        for t in range(frames):
            b1[t, 0:cols, 0:c1] = jnp.zeros((cols, c1), bf16)
        got[0] = jnp.zeros(got.shape[1:], f32)

    @pl.when(is_last)
    def _():
        for t in range(frames):
            b1[t, 0:cols, 2 * c1 : 3 * c1] = jnp.zeros((cols, c1), bf16)
        got[1] = jnp.zeros(got.shape[1:], f32)

    row_id = lax.broadcasted_iota(jnp.int32, (cols, 1), 0)
    lanes = g_ref.shape[-1]
    for t in range(frames):
        g = g_ref[t].astype(f32)
        left = jnp.where(row_id == 0, 0.0, pltpu.roll(g, 1, 0))
        right = jnp.where(row_id == cols - 1, 0.0, pltpu.roll(g, cols - 1, 0))
        gs[t, :, 0:lanes] = left.astype(bf16)
        gs[t, :, lanes : 2 * lanes] = g.astype(bf16)
        gs[t, :, 2 * lanes : 3 * lanes] = right.astype(bf16)

    for a in range(3):
        win[a] = jnp.zeros(win.shape[1:], bf16)
    copies[0].wait()
    for a in range(3):
        for e in range(3):
            for b in range(3):
                block = raw_in[a, b, e]
                for slot in range(3):
                    at = e * lanes + (slot + b) * c0
                    win[a, at : at + c0, slot * c1 : (slot + 1) * c1] = block

    copies[1].wait()
    for slot in range(2):
        for in_row in range(2):
            mixed = []
            for e in range(3):
                if slot == 0:
                    taps = (0, 1) if in_row == 0 else (2,)
                else:
                    taps = (0,) if in_row == 0 else (1, 2)
                value = raw_up[taps[0], e].astype(f32)
                for b in taps[1:]:
                    value = value + raw_up[b, e].astype(f32)
                mixed.append(value)
            k0, k1, k2 = mixed
            for parity in range(2):
                pair = (k0 + k1, k2) if parity == 0 else (k0, k1 + k2)
                at = parity * 2 * c2 + slot * c2
                for in_col in range(2):
                    wup[in_col, at : at + c2, in_row * c1 : (in_row + 1) * c1] = pair[in_col].astype(bf16)

    for a in range(3):
        wlow[a] = jnp.zeros(wlow.shape[1:], bf16)
    copies[2].wait()
    for a in range(3):
        for e in range(3):
            for b in range(3):
                block = raw_low[a, b, e]
                for q in range(2):
                    at = (4 * e + q + b) * c2
                    lane = q * (wlow.shape[-1] // 2)
                    wlow[a, at : at + c2, lane : lane + c3] = block

    for b in range(3):
        keep = None if b == 1 else (has_up if b == 0 else has_down).astype(f32)
        for t in range(frames):
            total = None
            for a in range(3):
                s = t + a - 2
                if s >= 0:
                    d = dot(gs[s], win[a, :, b * c1 : (b + 1) * c1])
                    total = d if total is None else total + d
            if b == 1:
                first_mid[t] = total
            act = rms_act(total, g1)
            if keep is not None:
                act = act * keep
            left = jnp.where(row_id == 0, 0.0, pltpu.roll(act, 1, 0))
            right = jnp.where(row_id == cols - 1, 0.0, pltpu.roll(act, cols - 1, 0))
            base = 3 * b * c1
            a1[t, :, base : base + c1] = left.astype(bf16)
            a1[t, :, base + c1 : base + 2 * c1] = act.astype(bf16)
            a1[t, :, base + 2 * c1 : base + 3 * c1] = right.astype(bf16)

    def halo(t, down):
        lane = 0 if down else 2 * c1
        peer = me + 1 if down else me - 1
        return pltpu.make_async_remote_copy(
            src_ref=sent.at[t],
            dst_ref=b1.at[t, pl.ds(0, cols), pl.ds(lane, c1)],
            send_sem=send_sem.at[int(down), t],
            recv_sem=recv_sem.at[int(down), t],
            device_id={"row": peer},
            device_id_type=pl.DeviceIdType.MESH,
        )

    waited = set()
    for t in range(frames):
        total = first_mid[t]
        for i, a in enumerate((2, 1, 0)):
            s = t + a - 2
            if s >= 0:
                if a not in waited:
                    waited.add(a)
                    copies[3 + i].wait()
                total = total + dot(a1[s], wmid[a])
        act = rms_act(total, g2).astype(bf16)
        sent[t] = act
        b1[t, 0:cols, c1 : 2 * c1] = act

        @pl.when(has_down)
        def _(t=t):
            halo(t, True).start()

        @pl.when(has_up)
        def _(t=t):
            halo(t, False).start()

    for i, a in enumerate((2, 1, 0)):
        if a not in waited:
            copies[3 + i].wait()

    lane3 = lax.broadcasted_iota(jnp.int32, (1, 2 * c2), 1)
    low3 = lane3 < c2
    tall_id = lax.broadcasted_iota(jnp.int32, (tall, 1), 0)
    keep_up, keep_down = has_up.astype(f32), has_down.astype(f32)
    lane4 = lax.broadcasted_iota(jnp.int32, (1, cols), 1)
    block = ys.shape[2] // 9

    def send_part(t, down):
        peer = me + 1 if down else me - 1
        return pltpu.make_async_remote_copy(
            src_ref=part.at[0 if down else 1, t],
            dst_ref=got.at[0 if down else 1, t],
            send_sem=psend.at[int(down), t],
            recv_sem=precv.at[int(down), t],
            device_id={"row": peer},
            device_id_type=pl.DeviceIdType.MESH,
        )

    for t in range(frames):
        @pl.when(has_up)
        def _(t=t):
            halo(t, True).wait_recv()

        @pl.when(has_down)
        def _(t=t):
            halo(t, False).wait_recv()

        b0[t] = pltpu.roll(b1[t].astype(f32), 1, 0).astype(bf16)
        for p in range(2):
            span = slice(p * c1, p * c1 + 2 * c1)
            third = dot_t(b0[t, :, span], wup[0]) + dot_t(b1[t, :, span], wup[1])
            for parity in range(2):
                field = third[:, parity * 2 * c2 : (parity + 1) * 2 * c2]
                act = pair_norm(field, g3, low3)
                edge = keep_up if p == 0 else keep_down
                outer = low3 if p == 0 else jnp.logical_not(low3)
                act = act * jnp.where(outer, edge, 1.0)
                drop = 0 if parity == 0 else cols
                act = jnp.where(tall_id == drop, 0.0, act)
                base = parity * 4 * c2 + p * 2 * c2
                a3[t, :, base : base + 2 * c2] = act.astype(bf16)
                a3s[t, :, base : base + 2 * c2] = pltpu.roll(act, tall - 1, 0).astype(bf16)

        for parity in range(2):
            total = None
            for a in range(3):
                s = t + a - 2
                if s < 0:
                    continue
                if parity == 0:
                    d = dot(a3[s, 0:cols, :], wlow[a, 0 : 8 * c2, :])
                    d += dot(a3s[s, 0:cols, 0 : 4 * c2], wlow[a, 8 * c2 : 12 * c2, :])
                else:
                    d = dot(a3[s, 0:cols, 4 * c2 : 8 * c2], wlow[a, 0 : 4 * c2, :])
                    d += dot(a3s[s, 0:cols, :], wlow[a, 4 * c2 : 12 * c2, :])
                total = d if total is None else total + d
            acts = []
            half = total.shape[-1] // 2
            for q in range(2):
                field = total[:, q * half : (q + 1) * half]
                mean = jnp.sum(field * field, axis=-1, keepdims=True) / c3
                acts.append(silu(field * lax.rsqrt(mean + eps) * g4).astype(bf16))
            act = jnp.concatenate(acts, axis=-1)
            ys[t, parity] = lax.dot_general(
                wout_ref[...], act, (((1,), (1,)), ((), ())), preferred_element_type=f32
            )

        even, odd = None, None
        for a in range(3):
            s = t + a - 2
            if s < 0:
                continue
            taps = [[ys[s, parity, (3 * a + e) * block : (3 * a + e + 1) * block, :] for e in range(3)] for parity in range(2)]
            before = jnp.where(lane4 == 0, 0.0, pltpu.roll(taps[1][0], 1, 1))
            after = jnp.where(lane4 == cols - 1, 0.0, pltpu.roll(taps[0][2], cols - 1, 1))
            new_even = before + taps[0][1] + taps[1][2]
            new_odd = taps[0][0] + taps[1][1] + after
            even = new_even if even is None else even + new_even
            odd = new_odd if odd is None else odd + new_odd
        rows = block // 4
        for parity, value in enumerate((even, odd)):
            part[1, t, parity] = value[0:rows]
            part[0, t, parity] = value[3 * rows : 4 * rows]
            out_ref[t, parity] = value[rows : 3 * rows]

        @pl.when(has_down)
        def _(t=t):
            send_part(t, True).start()

        @pl.when(has_up)
        def _(t=t):
            send_part(t, False).start()

    for t in range(frames):
        @pl.when(has_up)
        def _(t=t):
            send_part(t, True).wait_recv()
            halo(t, False).wait_send()
            send_part(t, False).wait_send()

        @pl.when(has_down)
        def _(t=t):
            send_part(t, False).wait_recv()
            halo(t, True).wait_send()
            send_part(t, True).wait_send()

        rows = block // 4
        for parity in range(2):
            out_ref[t, parity, 0:rows] += got[0, t, parity]
            out_ref[t, parity, rows : 2 * rows] += got[1, t, parity]


def per_device(latent, w_in, gain_one, w_mid, gain_two, w_up, gain_three, w_low, gain_four, w_out):
    frames, height, tw, c0 = latent.shape
    devices = lax.axis_size("row")
    cols = tw * devices
    assert height == devices
    c1, c2, c3 = w_in.shape[-1], w_up.shape[-1], w_low.shape[-1]
    colours = w_out.shape[-1]
    tall = cols + 16
    half, rows = 128, 8

    flat = jnp.transpose(latent, (1, 0, 2, 3)).reshape(height, frames, tw * c0)
    padded = jnp.pad(flat, ((2, 2), (0, 0), (0, 0)))
    blocks = jnp.stack([padded[s : s + height] for s in range(5)], axis=1)
    arrived = lax.all_to_all(blocks, "row", split_axis=0, concat_axis=0, tiled=True)
    g = arrived.reshape(devices, 5, frames, tw, c0)
    g = jnp.transpose(g, (2, 0, 3, 1, 4)).reshape(frames, cols, 5 * c0)
    lanes = -(-5 * c0 // 128) * 128
    g = jnp.pad(g, ((0, 0), (0, 0), (0, lanes - 5 * c0)))

    wmid = w_mid.reshape(3, 9 * c1, c1)
    wup = jnp.transpose(w_up, (0, 1, 3, 2))

    tap = jnp.transpose(w_out, (0, 2, 1, 4, 3))
    tap = jnp.pad(tap, ((0, 0), (0, 0), (0, 0), (0, rows - colours), (0, half - c3)))
    zero = jnp.zeros((3, 3, rows, half), bf16)
    by_slot = []
    for slot in range(4):
        sides = []
        for q in range(2):
            b = q - slot + 2
            sides.append(tap[:, :, b] if 0 <= b <= 2 else zero)
        by_slot.append(jnp.concatenate(sides, axis=-1))
    wout = jnp.stack(by_slot, axis=2).reshape(9 * 4 * rows, 2 * half)

    longest = max(c1, 2 * c2)
    gain_rows = (gain_one, gain_two, jnp.concatenate([gain_three, gain_three]), gain_four)
    gains = jnp.stack([jnp.pad(v, (0, longest - v.shape[0])) for v in gain_rows])

    vmem = pl.BlockSpec(memory_space=pltpu.VMEM)
    any_space = pl.BlockSpec(memory_space=pl.ANY)
    out = pl.pallas_call(
        functools.partial(kernel, (frames, cols, c0, c1, c2, c3, tall), devices),
        out_shape=jax.ShapeDtypeStruct((frames, 2, 2 * rows, cols), f32),
        in_specs=[vmem] * 2 + [any_space] * 4 + [vmem],
        out_specs=vmem,
        scratch_shapes=[
            pltpu.VMEM(w_in.shape, bf16),
            pltpu.VMEM(wup.shape, bf16),
            pltpu.VMEM(w_low.shape, bf16),
            pltpu.VMEM((3, 3 * lanes, 3 * c1), bf16),
            pltpu.VMEM(wmid.shape, bf16),
            pltpu.VMEM((2, 4 * c2, 2 * c1), bf16),
            pltpu.VMEM((3, 12 * c2, 2 * half), bf16),
            pltpu.VMEM((frames, cols, 3 * lanes), bf16),
            pltpu.VMEM((frames, cols, 9 * c1), bf16),
            pltpu.VMEM((frames, cols, c1), f32),
            pltpu.VMEM((frames, tall, 3 * c1), bf16),
            pltpu.VMEM((frames, tall, 3 * c1), bf16),
            pltpu.VMEM((frames, cols, c1), bf16),
            pltpu.VMEM((frames, tall, 8 * c2), bf16),
            pltpu.VMEM((frames, tall, 8 * c2), bf16),
            pltpu.VMEM((frames, 2, 9 * 4 * rows, cols), f32),
            pltpu.VMEM((2, frames, 2, rows, cols), f32),
            pltpu.VMEM((2, frames, 2, rows, cols), f32),
            pltpu.SemaphoreType.DMA((6,)),
            pltpu.SemaphoreType.DMA((2, frames)),
            pltpu.SemaphoreType.DMA((2, frames)),
            pltpu.SemaphoreType.DMA((2, frames)),
            pltpu.SemaphoreType.DMA((2, frames)),
        ],
        compiler_params=pltpu.CompilerParams(
            collective_id=0, has_side_effects=True, vmem_limit_bytes=60 * 1024 * 1024
        ),
    )(
        g, gains, w_in, wmid, wup, w_low, wout,
    )
    out = out.reshape(frames, 2, 2, rows, cols)[:, :, :, :colours]
    return jnp.transpose(out, (0, 3, 2, 4, 1)).reshape(frames, colours, 2, 2 * cols)


def solution(mesh):
    placed = (P("groups", None, "row", None), P(), P(), P(), P(), P(), P(), P(), P(), P())
    return jax.shard_map(
        per_device,
        mesh=mesh,
        in_specs=placed,
        out_specs=P("groups", None, "row", None),
        check_vma=False,
    )
```

profile of v0, /device:TPU:0, one launch (start us, length us, event | category | flops | bytes accessed | tf_op | source)
XLA Modules:
  0.0 52.7 jit_solution(8986383980854028317)
XLA Ops:
  0.0 1.0 %copy.21 = bf16[16,4,8,16]{3,2,1,0:T(8,128)(2,1)S(1)} copy(bf16[16,4,8,16]{3,2,0,1:T(8,128)(2,1)} %bitcast.56) | data formatting | bytes 32768 | tf_op jit(solution)/shard_map/transpose | solution.py:326
  1.0 0.1 reshape.22
  1.1 0.1 stack.50
  1.3 0.6 %bitcast_dynamic-update-slice_fusion.2 = bf16[16,5,4,128]{3,2,1,0:T(4,128)(2,1)} fusion(bf16[16,4,128]{2,1,0:T(4,128)(2,1)S(1)} %reshape.22), kind=kLoop, calls=%fused_computation.13 | loop fusion | bytes 32768
  1.9 0.6 %bitcast_dynamic-update-slice_fusion.1 = bf16[16,5,4,128]{3,2,1,0:T(4,128)(2,1)} fusion(bf16[16,5,4,128]{3,2,1,0:T(4,128)(2,1)} %bitcast_dynamic-update-slice_fusion.2, bf16[16,4,128]{2,1,0:T(4,128)(2,1)S(1)} %reshape.22), kind=kLoop, calls=%fused_computation.12 | loop fusion | bytes 32768
  2.5 0.6 %constant_dynamic-update-slice_fusion = bf16[16,5,4,128]{3,2,1,0:T(4,128)(2,1)} fusion(bf16[16,5,4,128]{3,2,1,0:T(4,128)(2,1)} %bitcast_dynamic-update-slice_fusion.1, bf16[16,1,4,128]{3,2,1,0:T(4,128)(2,1)S(1)} %stack.50), kind=kLoop, calls=%fused_computation.15 | loop fusion | bytes 32768
  3.1 0.6 %bitcast_dynamic-update-slice_fusion = bf16[16,5,4,128]{3,2,1,0:T(4,128)(2,1)} fusion(bf16[16,5,4,128]{3,2,1,0:T(4,128)(2,1)} %constant_dynamic-update-slice_fusion, bf16[16,4,128]{2,1,0:T(4,128)(2,1)S(1)} %reshape.22), kind=kLoop, calls=%fused_computation.11 | loop fusion | bytes 32768
  3.7 0.6 %bitcast_dynamic-update-slice_fusion.3 = bf16[16,5,4,128]{3,2,1,0:T(4,128)(2,1)} fusion(bf16[16,5,4,128]{3,2,1,0:T(4,128)(2,1)} %bitcast_dynamic-update-slice_fusion, bf16[16,4,128]{2,1,0:T(4,128)(2,1)S(1)} %reshape.22), kind=kLoop, calls=%fused_computation.14 | loop fusion | bytes 32768 | tf_op jit(solution)/shard_map/stack | solution.py:328
  4.3 7.4 %all-to-all-start = ((bf16[16,5,4,128]{3,2,1,0:T(4,128)(2,1)}), bf16[16,5,4,128]{3,2,1,0:T(4,128)(2,1)S(1)}, u32[]{:S(2)}, u32[]{:S(2)}) async-start(bf16[16,5,4,128]{3,2,1,0:T(4,128)(2,1)} %bitcast_dynamic-update-slice_fusion.3), calls=%async_computation | async-start | bytes 163840 | tf_op jit(solution)/shard_map/all_to_all | solution.py:329
  11.8 0.8 %fusion.2 = (bf16[3,3,8,128]{3,2,1,0:T(8,128)(2,1)S(1)}, bf16[3,3,8,128]{3,2,1,0:T(8,128)(2,1)S(1)}, bf16[3,3,8,128]{3,2,1,0:T(8,128)(2,1)S(1)}) fusion(bf16[3,3,3,3,96]{4,3,1,2,0:T(4,128)(2,1)} %bitcast.57), kind=kLoop, calls=%fused_computation.10 | loop fusion | bytes 70848 | tf_op jit(solution)/shard_map/squeeze | solution.py:346
  12.6 0.0 copy-done.2
  12.6 0.1 pad_maximum_fusion.2
  12.7 0.0 copy-done.3
  12.7 0.7 %copy.30 = bf16[3,3,4,8,256]{4,3,2,1,0:T(8,128)(2,1)} copy(bf16[3,3,4,8,256]{4,3,1,0,2:T(8,128)(2,1)S(1)} %pad_maximum_fusion) | data formatting | bytes 294912 | tf_op jit(solution)/shard_map/stack | solution.py:348
  13.4 0.6 %pad_maximum_fusion.1.gains_ref = f32[4,384]{1,0:T(4,128)} fusion(f32[1,384]{1,0:T(1,128)S(1)} %stack.57, f32[1,384]{1,0:T(1,128)S(1)} %stack.56, f32[1,384]{1,0:T(1,128)S(1)} %stack.55, f32[1,384]{1,0:T(1,128)S(1)} %stack.54), kind=kLoop, calls=%fused_computation.16 | loop fusion | flops 4608 | bytes 12288 | tf_op jit(solution)/shard_map/stack | solution.py:352
  14.0 4.9 %all-to-all-done = bf16[16,5,4,128]{3,2,1,0:T(4,128)(2,1)S(1)} async-done(((bf16[16,5,4,128]{3,2,1,0:T(4,128)(2,1)}), bf16[16,5,4,128]{3,2,1,0:T(4,128)(2,1)S(1)}, u32[]{:S(2)}, u32[]{:S(2)}) %all-to-all-start) | async-done | bytes 81952 | tf_op jit(solution)/shard_map/all_to_all | solution.py:329
  18.9 0.4 reshape.23
  19.3 0.8 %copy.27 = bf16[4,16,8,5,16]{4,3,2,1,0:T(8,128)(2,1)S(1)} copy(bf16[4,16,8,5,16]{4,2,1,0,3:T(8,128)(2,1)S(1)} %bitcast.52) | data formatting | bytes 163840 | tf_op jit(solution)/shard_map/transpose | solution.py:331
  20.2 0.5 reshape.24
  20.7 0.7 %pad.19.g_ref = bf16[4,128,128]{2,1,0:T(8,128)(2,1)} pad(bf16[4,128,80]{2,1,0:T(8,128)(2,1)S(1)} %reshape.24, bf16[]{:T(256)} %constant.4.clone.1), padding=0_0x0_0x0_48 | pad | bytes 212994 | tf_op jit(solution)/shard_map/jit(_pad)/pad | solution.py:333
  21.4 29.1 %shard_map.100 = f32[4,2,16,128]{3,2,1,0:T(8,128)} custom-call(bf16[4,128,128]{2,1,0:T(8,128)(2,1)} %pad.19.g_ref, f32[4,384]{1,0:T(4,128)} %pad_maximum_fusion.1.gains_ref, bf16[3,3,3,16,384]{4,3,2,1,0:T(8,128)(2,1)} %win_hbm.1, bf16[3,3456,384]{2,1,0:T(8,128)(2,1)} %bitcast.50, bf16[3,3,192,384]{3,2,1,0:T(8,128)(2,1)} %bitcast.53, ...), custom_call_target="tpu_custom_call" | custom-call | tf_op jit(solution)/shard_map/pallas_call | solution.py:356
  50.5 0.8 %slice.36 = f32[4,2,2,3,128]{4,3,2,1,0:T(4,128)S(1)} slice(f32[4,2,2,8,128]{4,3,2,1,0:T(8,128)} %bitcast.55), slice={[0:4], [0:2], [0:2], [0:3], [0:128]} | slice | bytes 49152 | tf_op jit(solution)/shard_map/slice | solution.py:392
  51.4 0.5 copy.35
  51.8 0.9 %copy.32 = f32[4,3,2,256]{3,2,1,0:T(2,128)} copy(f32[4,3,2,256]{0,3,2,1:T(8,128)S(1)} %bitcast.51) | data formatting | bytes 49152 | tf_op jit(solution)/shard_map/reshape | solution.py:393
  (14 shorter events, 0.1 us)
Async XLA Ops:
  0.0 12.6 %copy-start.2 = (f32[192]{0:T(256)S(1)}, f32[192]{0:T(256)}, u32[]{:S(2)}) copy-start(f32[192]{0:T(256)} %param.16) | copy-start | bytes 2308
  0.0 12.7 %copy-start.3 = (f32[96]{0:T(128)S(1)}, f32[96]{0:T(128)}, u32[]{:S(2)}) copy-start(f32[96]{0:T(128)} %param.18) | copy-start | bytes 1156
  0.0 12.7 %copy-start = (f32[384]{0:T(512)S(1)}, f32[384]{0:T(512)}, u32[]{:S(2)}) copy-start(f32[384]{0:T(512)} %param.14) | copy-start | bytes 4612
  0.0 12.7 %copy-start.1 = (f32[384]{0:T(512)S(1)}, f32[384]{0:T(512)}, u32[]{:S(2)}) copy-start(f32[384]{0:T(512)} %param.12) | copy-start | bytes 4612
  4.3 14.5 %all-to-all-start = ((bf16[16,5,4,128]{3,2,1,0:T(4,128)(2,1)}), bf16[16,5,4,128]{3,2,1,0:T(4,128)(2,1)S(1)}, u32[]{:S(2)}, u32[]{:S(2)}) async-start(bf16[16,5,4,128]{3,2,1,0:T(4,128)(2,1)} %bitcast_dynamic-update-slice_fusion.3), calls=%async_computation | async-start | bytes 163840 | tf_op jit(solution)/shard_map/all_to_all | solution.py:329
where the time goes:
time: 53.4 us; the launch traced here: 52.7 us
  Pallas kernels  29.1 us (54%)
  local copies, waits for them, and re-layouts  10.4 us (19%)
  starting transfers between devices  7.41 us (14%)
  waiting for transfers between devices  4.88 us (9%)
  other arithmetic  0.72 us (1%)
    pallas_call x1, Pallas kernels, per_device(): pl.pallas_call(functools.partial(kernel, (frames, cols, c0, c1, c2, c3, t...  29.1 us
    all_to_all x1, starting transfers between devices, per_device(): lax.all_to_all(blocks, 'row', split_axis=0, concat_axis=0, tiled=True)  7.41 us
    all_to_all x1, waiting for transfers between devices, per_device(): lax.all_to_all(blocks, 'row', split_axis=0, concat_axis=0, tiled=True)  4.88 us
    unnamed x13, local copies, waits for them, and re-layouts  2.96 us
  transfers between devices with their start and end apart: 1, of which 1 were waited for; matrix products, arithmetic and copies ran while one was open for 4% of the time, Pallas kernels for 0%

commit v1 on v0

v1 whole, which is shorter than its diff:
```python
import functools

import jax
import jax.numpy as jnp
from jax import lax
from jax.experimental import pallas as pl
from jax.experimental.pallas import tpu as pltpu
from jax.sharding import PartitionSpec as P

eps = 1e-06
f32, bf16, i32 = jnp.float32, jnp.bfloat16, jnp.int32
MESH = pl.DeviceIdType.MESH
LANES = 128


def half_silu(h):
    return h * jnp.tanh(h) + h


def rms_act(field, half_gain, count):
    mean = jnp.sum(field * field, axis=-1, keepdims=True) * (1.0 / count)
    return half_silu(field * lax.rsqrt(mean + eps) * half_gain)


def pair_norm(field, half_gain, low):
    half = field.shape[-1] // 2
    square = field * field
    first = jnp.sum(jnp.where(low, square, 0.0), axis=-1, keepdims=True)
    second = jnp.sum(jnp.where(low, 0.0, square), axis=-1, keepdims=True)
    inv = 1.0 / half
    scale = jnp.where(low, lax.rsqrt(first * inv + eps), lax.rsqrt(second * inv + eps))
    return half_silu(field * scale * half_gain)


def dot(a, b):
    return jnp.dot(a, b, preferred_element_type=f32)


def iota(shape, axis):
    return lax.broadcasted_iota(i32, shape, axis)


def merge(value):
    return value.reshape(-1, value.shape[-1])


def rows_of(value, count):
    return value.reshape(count, value.shape[0] // count, value.shape[1])


def kernel(
    sizes, devices, packed,
    lat_hbm, g1_ref, g2_ref, g3_ref, g4_ref,
    win_hbm, wmid_hbm, wup_hbm, wlow_hbm, wout_hbm,
    out_ref,
    raw_lat, lat_t, raw_in, raw_up, raw_low, raw_out,
    win, wmid, wupt, wup, wlow, wout_rows, wo, spread, g3x, g4x,
    latx, xs, first, a1, b1, b0, a3, act4, part, got, got_rows,
    wsem, lsend, lrecv, hsend, hrecv, psend, precv,
):
    frames, height, cw, c0, c1, c2, c3, colours = sizes
    ext = cw + 2
    wide = 2 * cw
    nc = wide + 2
    fc = frames * c0
    kinds = 2 * colours
    me = lax.axis_index("row")
    is_first, is_last = me == 0, me == devices - 1
    has_left, has_right = me > 0, me < devices - 1

    copies = {}

    def load(name, src, dst, k):
        copies[name] = pltpu.make_async_copy(src, dst, wsem.at[k])
        copies[name].start()

    load("lat", lat_hbm, latx.at[pl.ds(2, cw)] if packed else raw_lat, 0)
    load("in", win_hbm, raw_in, 1)
    load("out", wout_hbm, raw_out, 2)
    load("up", wup_hbm, raw_up, 3)
    load("low", wlow_hbm, raw_low, 4)
    for a in range(3):
        for b in range(3):
            load(("mid", a, b), wmid_hbm.at[a, b], wmid.at[:, b, :, pl.ds(a * c1, c1)], 5 + 3 * a + b)

    barrier = pltpu.get_barrier_semaphore()

    def greet(k, _):
        pl.semaphore_signal(barrier, inc=1, device_id={"row": lax.rem(me + k, devices)}, device_id_type=MESH)
        return _

    lax.fori_loop(1, devices, greet, 0)

    copies["lat"].wait()
    if not packed:
        chan, lane = iota((c0, LANES), 0), iota((c0, LANES), 1)
        total = None
        for t in range(frames):
            put = ((lane == t * c0 + chan) | (lane == fc + t * c0 + chan)).astype(bf16)
            field = raw_lat[t].astype(f32).reshape(height * cw, c0).astype(bf16)
            d = dot(field, put)
            total = d if total is None else total + d
        lat_t[...] = total
        for j in range(cw):
            latx[2 + j] = lat_t[pl.ds(j, height, stride=cw), :].astype(bf16)

    pl.semaphore_wait(barrier, devices - 1)

    def lat_copy(right):
        peer = me + 1 if right else me - 1
        src = latx.at[pl.ds(cw, 2)] if right else latx.at[pl.ds(2, 2)]
        dst = latx.at[pl.ds(0, 2)] if right else latx.at[pl.ds(cw + 2, 2)]
        return pltpu.make_async_remote_copy(
            src_ref=src, dst_ref=dst, send_sem=lsend.at[int(right)], recv_sem=lrecv.at[int(right)],
            device_id={"row": peer}, device_id_type=MESH,
        )

    @pl.when(has_right)
    def _():
        lat_copy(True).start()

    @pl.when(has_left)
    def _():
        lat_copy(False).start()

    @pl.when(is_first)
    def _():
        latx[0:2] = jnp.zeros((2, height, LANES), bf16)
        for t in range(frames):
            b1[t, 0] = jnp.zeros((height, c1), bf16)

    @pl.when(is_last)
    def _():
        latx[cw + 2 : cw + 4] = jnp.zeros((2, height, LANES), bf16)
        for t in range(frames):
            b1[t, ext - 1] = jnp.zeros((height, c1), bf16)

    copies["in"].wait()
    kx = 2 * LANES
    for e in range(3):
        for b in range(3):
            for s in range(frames):
                at = e * kx + b * fc + s * c0
                for t in range(frames):
                    a = s - t + 2
                    block = raw_in[a, b, e] if 0 <= a <= 2 else jnp.zeros((c0, c1), bf16)
                    win[at : at + c0, t * c1 : (t + 1) * c1] = block
        win[e * kx + 3 * fc : (e + 1) * kx, :] = jnp.zeros((kx - 3 * fc, frames * c1), bf16)

    hg1, hg2 = g1_ref[...] * 0.5, g2_ref[...] * 0.5
    g3x[0:1, 0:c2] = g3_ref[...] * 0.5
    g3x[0:1, c2 : 2 * c2] = g3_ref[...] * 0.5
    g4x[...] = jnp.zeros(g4x.shape, f32)
    g4x[0:1, 0:c3] = g4_ref[...] * 0.5

    copies["up"].wait()
    for row_odd in range(2):
        for in_row in range(2):
            mixed = []
            for e in range(3):
                if row_odd == 0:
                    taps = (0, 1) if in_row == 0 else (2,)
                else:
                    taps = (0,) if in_row == 0 else (1, 2)
                value = raw_up[taps[0], e].astype(f32)
                for b in taps[1:]:
                    value = value + raw_up[b, e].astype(f32)
                mixed.append(value)
            k0, k1, k2 = mixed
            for parity in range(2):
                pair = (k0 + k1, k2) if parity == 0 else (k0, k1 + k2)
                at = parity * 2 * c2 + row_odd * c2
                for in_col in range(2):
                    wupt[in_row, at : at + c2, in_col * c1 : (in_col + 1) * c1] = pair[in_col].astype(bf16)
    for in_row in range(2):
        for i in range(0, 4 * c2, LANES):
            for j in range(0, 2 * c1, LANES):
                wup[in_row, j : j + LANES, i : i + LANES] = wupt[in_row, i : i + LANES, j : j + LANES].T

    copies["low"].wait()
    for a in range(3):
        wlow[a] = jnp.zeros(wlow.shape[1:], bf16)
        for e in range(3):
            for b in range(3):
                block = raw_low[a, b, e]
                for q in range(2):
                    at = (4 * e + q + b) * c2
                    wlow[a, at : at + c2, q * LANES : q * LANES + c3] = block

    copies["out"].wait()
    tap_rows = wout_rows.shape[1]
    wout_rows[...] = jnp.zeros(wout_rows.shape, f32)
    for a in range(3):
        for b in range(3):
            for e in range(3):
                at = (3 * b + e) * colours
                wout_rows[a, at : at + colours, 0:c3] = raw_out[a, b, e].astype(f32)
    lane = iota((1, 6 * LANES), 1)
    tap_col = lane // (2 * LANES)
    group = (lane // LANES) % 2
    spot = lane % LANES
    kind = spot // nc
    row_kind, colour = kind // colours, kind % colours
    slot = jnp.where(group == 0, 1 + row_kind, 3 - 3 * row_kind)
    tap = iota((tap_rows, 6 * LANES), 0)
    for q in range(2):
        b = q - slot + 2
        wanted = jnp.where((b >= 0) & (b <= 2) & (kind < kinds), (3 * b + tap_col) * colours + colour, -1)
        select = (tap == wanted).astype(bf16)
        for a in range(3):
            wo[a, q * LANES : (q + 1) * LANES, :] = lax.dot_general(
                wout_rows[a].astype(bf16), select, (((0,), (0,)), ((), ())), preferred_element_type=f32
            ).astype(bf16)

    full = wide * devices
    spot = iota((LANES, full), 0)
    col = iota((LANES, full), 1) % wide
    for k in range(kinds):
        spread[:, k * full : (k + 1) * full] = (spot == k * nc + 1 + col).astype(bf16)

    @pl.when(has_left)
    def _():
        lat_copy(True).wait_recv()

    @pl.when(has_right)
    def _():
        lat_copy(False).wait_recv()

    h3 = iota((1, height, 1), 1)
    top3, bottom3 = h3 == 0, h3 == height - 1
    low_lanes = iota((1, 1, LANES), 2) < fc
    for j in range(0, cw + 4, 2):
        v = latx[j : j + 2].astype(f32)
        up = jnp.where(top3, 0.0, pltpu.roll(v, 1, 1))
        down = jnp.where(bottom3, 0.0, pltpu.roll(v, height - 1, 1))
        xs[j : j + 2, :, 0:LANES] = jnp.where(low_lanes, up, v).astype(bf16)
        xs[j : j + 2, :, LANES:kx] = jnp.where(low_lanes, down, 0.0).astype(bf16)

    lhs = jnp.concatenate([merge(xs[e : e + ext]) for e in range(3)], axis=-1)
    keep_left, keep_right = has_left.astype(f32), has_right.astype(f32)
    col_id = iota((ext * height, 1), 0)
    keep = jnp.where(col_id < height, keep_left, jnp.where(col_id >= (ext - 1) * height, keep_right, 1.0))
    for t in range(frames):
        total = dot(lhs, win[:, t * c1 : (t + 1) * c1])
        first[t] = total[height : (cw + 1) * height]
        act = rows_of(rms_act(total, hg1, c1) * keep, ext)
        up = jnp.where(top3, 0.0, pltpu.roll(act, 1, 1))
        down = jnp.where(bottom3, 0.0, pltpu.roll(act, height - 1, 1))
        a1[t, :, :, 0:c1] = up.astype(bf16)
        a1[t, :, :, c1 : 2 * c1] = act.astype(bf16)
        a1[t, :, :, 2 * c1 : 3 * c1] = down.astype(bf16)

    for a in range(3):
        for b in range(3):
            copies[("mid", a, b)].wait()

    def halo(t, right):
        peer = me + 1 if right else me - 1
        return pltpu.make_async_remote_copy(
            src_ref=b1.at[t, cw if right else 1], dst_ref=b1.at[t, 0 if right else ext - 1],
            send_sem=hsend.at[int(right), t], recv_sem=hrecv.at[int(right), t],
            device_id={"row": peer}, device_id_type=MESH,
        )

    sums = {t: [] for t in range(frames)}
    groups = [list(range(frames - 2)), [frames - 2], [frames - 1]]
    m = cw * height
    for group_of in groups:
        s0, n = group_of[0], len(group_of)
        least = max(0, 3 - (frames - s0))
        lhs = jnp.concatenate([merge(a1[s0 : s0 + n, e : e + cw]) for e in range(3)], axis=-1)
        d = dot(lhs, merge(wmid[:, :, :, least * c1 : 3 * c1]))
        for i, s in enumerate(group_of):
            for a in range(least, 3):
                t = s - a + 2
                sums[t].append(d[i * m : (i + 1) * m, (a - least) * c1 : (a - least + 1) * c1])
        for t in group_of:
            total = first[t]
            for v in sums[t]:
                total = total + v
            b1[t, 1 : cw + 1] = rows_of(rms_act(total, hg2, c1).astype(bf16), cw)

            @pl.when(has_right)
            def _(t=t):
                halo(t, True).start()

            @pl.when(has_left)
            def _(t=t):
                halo(t, False).start()

    low3 = iota((1, 2 * c2), 1) < c2
    pairs = cw + 1
    tall = iota((pairs * height, 1), 0)
    top = tall % height == 0
    bottom = tall % height == height - 1
    hg3, hg4 = g3x[...], g4x[...]

    def upsample(t):
        @pl.when(has_left)
        def _():
            halo(t, True).wait_recv()

        @pl.when(has_right)
        def _():
            halo(t, False).wait_recv()

        b0[t] = pltpu.roll(b1[t].astype(f32), 1, 1).astype(bf16)
        above = jnp.concatenate([merge(b0[t, e : e + pairs]) for e in range(2)], axis=-1)
        here = jnp.concatenate([merge(b1[t, e : e + pairs]) for e in range(2)], axis=-1)
        from_above, from_here = dot(above, wup[0]), dot(here, wup[1])
        for parity in range(2):
            span = slice(parity * 2 * c2, (parity + 1) * 2 * c2)
            field = jnp.where(top & ~low3, 0.0, from_above[:, span]) + jnp.where(top & low3, 0.0, from_here[:, span])
            act = pair_norm(field, hg3, low3)
            if parity == 0:
                act = act * jnp.where(tall < height, keep_left, 1.0)
            else:
                act = act * jnp.where(tall >= cw * height, keep_right, 1.0)
            act = rows_of(act, pairs)
            ahead = pltpu.roll(act, height - 1, 1)
            low = low3.reshape(1, 1, 2 * c2)
            a3[t, :, parity, :, 0 : 2 * c2] = jnp.where(top3 & low, 0.0, act).astype(bf16)
            a3[t, :, parity, :, 2 * c2 : 4 * c2] = jnp.where(bottom3 & ~low, 0.0, ahead).astype(bf16)

    lane_mod = iota((1, LANES), 1) % nc
    h2 = iota((height, 1), 0)
    even_kind = iota((1, LANES), 1) < colours * nc

    def message(t):
        def copy(k, act):
            peer = lax.rem(me + k, devices)
            return pltpu.make_async_remote_copy(
                src_ref=part.at[t, peer], dst_ref=got.at[t, me], send_sem=psend.at[t], recv_sem=precv.at[t],
                device_id={"row": peer}, device_id_type=MESH,
            )
        return copy

    def lower(t):
        total = None
        for a in range(3):
            s = t + a - 2
            if s < 0:
                continue
            field = a3[s].reshape(nc, height, 4 * c2)
            lhs = jnp.concatenate([merge(field[e : e + wide]) for e in range(3)], axis=-1)
            d = dot(lhs, wlow[a])
            total = d if total is None else total + d
        for q in range(2):
            span = slice(q * LANES, (q + 1) * LANES)
            act4[t, :, span] = rms_act(total[:, span], hg4, c3).astype(bf16)
        total = None
        for a in range(3):
            s = t + a - 2
            if s < 0:
                continue
            d = dot(act4[s], wo[a])
            total = d if total is None else total + d
        out = [None, None]
        for e in range(3):
            for c in range(wide):
                for g in range(2):
                    at = (2 * e + g) * LANES
                    v = jnp.where(lane_mod == c + 2 - e, total[c * height : (c + 1) * height, at : at + LANES], 0.0)
                    out[g] = v if out[g] is None else out[g] + v
        down = jnp.where(h2 == 0, 0.0, pltpu.roll(out[1], 1, 0))
        up = jnp.where(h2 == height - 1, 0.0, pltpu.roll(out[1], height - 1, 0))
        value = out[0] + jnp.where(even_kind, down, up)
        for d in range(devices):
            part[t, d] = value[d : d + 1]
        got[t, me] = part[t, me]

        def send(k, _):
            message(t)(k, None).start()
            return _

        lax.fori_loop(1, devices, send, 0)

    def all_sent(t, sem):
        return pltpu.make_async_copy(got.at[t, pl.ds(0, devices - 1)], got.at[t, pl.ds(0, devices - 1)], sem)

    source = iota((devices, 1), 0)
    cell = iota((devices, full), 1) // wide
    inside = (lane_mod >= 1) & (lane_mod <= wide)

    def finish(t):
        all_sent(t, precv.at[t]).wait()
        for d in range(devices):
            got_rows[d : d + 1] = got[t, d]
        g = got_rows[...]
        before = jnp.where((lane_mod == 0) & (source > 0), g, 0.0)
        after = jnp.where((lane_mod == nc - 1) & (source < devices - 1), g, 0.0)
        before = pltpu.roll(pltpu.roll(before, devices - 1, 0), wide, 1)
        after = pltpu.roll(pltpu.roll(after, 1, 0), LANES - wide, 1)
        g = jnp.where(inside, g, 0.0) + before + after
        high = g.astype(bf16)
        rest = g - high.astype(f32)
        middle = rest.astype(bf16)
        rest = rest - middle.astype(f32)
        d = dot(jnp.concatenate([high, middle, rest.astype(bf16)], axis=0), spread[...])
        d = d[0:devices] + d[devices : 2 * devices] + d[2 * devices : 3 * devices]
        for k in range(kinds):
            row = jnp.sum(jnp.where(cell == source, d[:, k * full : (k + 1) * full], 0.0), axis=0, keepdims=True)
            out_ref[t, k % colours, k // colours : k // colours + 1, :] = row

    for t in range(frames - 1):
        upsample(t)
    for t in range(frames - 1):
        lower(t)
    upsample(frames - 1)
    lower(frames - 1)
    for t in range(frames):
        finish(t)

    @pl.when(has_right)
    def _():
        lat_copy(True).wait_send()
        for t in range(frames):
            halo(t, True).wait_send()

    @pl.when(has_left)
    def _():
        lat_copy(False).wait_send()
        for t in range(frames):
            halo(t, False).wait_send()

    for t in range(frames):
        all_sent(t, psend.at[t]).wait()


def per_device(latent, w_in, gain_one, w_mid, gain_two, w_up, gain_three, w_low, gain_four, w_out):
    frames, height, cw, c0 = latent.shape
    devices = lax.axis_size("row")
    assert height == devices
    c1, c2, c3 = w_in.shape[-1], w_up.shape[-1], w_low.shape[-1]
    colours = w_out.shape[-1]
    ext, wide = cw + 2, 2 * cw
    full = wide * devices
    kinds = 2 * colours
    assert 2 * frames * c0 == LANES and kinds * (wide + 2) <= LANES
    packed = cw % 8 != 0
    if packed:
        lat = jnp.transpose(latent, (2, 1, 0, 3)).reshape(cw, height, frames * c0)
        lat = jnp.concatenate([lat, lat], axis=-1)
    else:
        lat = latent
    wup = jnp.transpose(w_up, (0, 1, 3, 2))
    wout = jnp.transpose(w_out, (0, 1, 2, 4, 3))
    tap_rows = -(-9 * colours // 16) * 16

    vmem = pl.BlockSpec(memory_space=pltpu.VMEM)
    hbm = pl.BlockSpec(memory_space=pl.ANY)
    dma = pltpu.SemaphoreType.DMA
    return pl.pallas_call(
        functools.partial(kernel, (frames, height, cw, c0, c1, c2, c3, colours), devices, packed),
        out_shape=jax.ShapeDtypeStruct((frames, colours, 2, full), f32),
        in_specs=[hbm] + [vmem] * 4 + [hbm] * 5,
        out_specs=vmem,
        scratch_shapes=[
            pltpu.VMEM(latent.shape, bf16),
            pltpu.VMEM((height * cw, LANES), f32),
            pltpu.VMEM(w_in.shape, bf16),
            pltpu.VMEM(wup.shape, bf16),
            pltpu.VMEM(w_low.shape, bf16),
            pltpu.VMEM(wout.shape, bf16),
            pltpu.VMEM((3 * 2 * LANES, frames * c1), bf16),
            pltpu.VMEM((3, 3, c1, 3 * c1), bf16),
            pltpu.VMEM((2, 4 * c2, 2 * c1), bf16),
            pltpu.VMEM((2, 2 * c1, 4 * c2), bf16),
            pltpu.VMEM((3, 12 * c2, 2 * LANES), bf16),
            pltpu.VMEM((3, tap_rows, LANES), f32),
            pltpu.VMEM((3, 2 * LANES, 6 * LANES), bf16),
            pltpu.VMEM((LANES, kinds * full), bf16),
            pltpu.VMEM((1, 2 * c2), f32),
            pltpu.VMEM((1, LANES), f32),
            pltpu.VMEM((cw + 4, height, LANES), bf16),
            pltpu.VMEM((cw + 4, height, 2 * LANES), bf16),
            pltpu.VMEM((frames, cw * height, c1), f32),
            pltpu.VMEM((frames, ext, height, 3 * c1), bf16),
            pltpu.VMEM((frames, ext, height, c1), bf16),
            pltpu.VMEM((frames, ext, height, c1), bf16),
            pltpu.VMEM((frames, cw + 1, 2, height, 4 * c2), bf16),
            pltpu.VMEM((frames, wide * height, 2 * LANES), bf16),
            pltpu.VMEM((frames, devices, 1, LANES), f32),
            pltpu.VMEM((frames, devices, 1, LANES), f32),
            pltpu.VMEM((devices, LANES), f32),
            dma((14,)), dma((2,)), dma((2,)), dma((2, frames)), dma((2, frames)), dma((frames,)), dma((frames,)),
        ],
        compiler_params=pltpu.CompilerParams(
            collective_id=0, has_side_effects=True, vmem_limit_bytes=60 * 1024 * 1024
        ),
    )(
        lat, gain_one.reshape(1, c1), gain_two.reshape(1, c1), gain_three.reshape(1, c2), gain_four.reshape(1, c3),
        w_in, w_mid, wup, w_low, wout,
    )


def solution(mesh):
    placed = (P("groups", None, "row", None), P(), P(), P(), P(), P(), P(), P(), P(), P())
    return jax.shard_map(
        per_device,
        mesh=mesh,
        in_specs=placed,
        out_specs=P("groups", None, "row", None),
        check_vma=False,
    )
```

time: 53.4 us -> 34.9 us (0.65)
  starting transfers between devices: 7.41 us -> 0 us
  local copies, waits for them, and re-layouts: 10.4 us -> 3.84 us
  waiting for transfers between devices: 4.88 us -> 0 us
  Pallas kernels: 29.1 us -> 30.9 us
  other arithmetic: 0.72 us -> 0 us
    all_to_all x1 -> x0, starting transfers between devices: 7.41 us -> none  [per_device(): lax.all_to_all(blocks, 'row', split_axis=0, concat_axis=0, tiled=True)]
    all_to_all x1 -> x0, waiting for transfers between devices: 4.88 us -> none  [per_device(): lax.all_to_all(blocks, 'row', split_axis=0, concat_axis=0, tiled=True)]
    transpose x2 -> x0, local copies, waits for them, and re-layouts: 1.8 us -> none  [the longest x1 0.98 us: per_device(): flat = jnp.transpose(latent, (1, 0, 2, 3)).reshape(height, frames, tw * c0)]
    pallas_call x1, Pallas kernels: 29.1 us -> 30.9 us  [per_device(): pl.pallas_call(functools.partial(kernel, (frames, height, cw, c0, c1, c2,...]
    unnamed x13 -> x1, local copies, waits for them, and re-layouts: 2.96 us -> 1.35 us
    another operation x7 -> x0, local copies, waits for them, and re-layouts: 1.42 us -> none  [the longest x2 0.74 us: per_device(): blocks = jnp.stack([padded[s:s + height] for s in range(5)], axis=1)]
    slice x1 -> x0, local copies, waits for them, and re-layouts: 0.85 us -> none  [per_device(): out = out.reshape(frames, 2, 2, rows, cols)[:, :, :, :colours]]
    squeeze x1 -> x0, local copies, waits for them, and re-layouts: 0.76 us -> none  [per_device(): sides.append(tap[:, :, b] if 0 <= b <= 2 else zero)]
  transfers between devices with their start and end apart: 1 -> 0, of which waited for: 1 -> 0; matrix products, arithmetic and copies ran while one was open for 4% -> 0% of each run, Pallas kernels for 0% -> 0%
where the time goes in v1:
time: 34.9 us; the launch traced here: 34.7 us
  Pallas kernels  30.9 us (89%)
  local copies, waits for them, and re-layouts  3.84 us (11%)
    pallas_call x1, Pallas kernels, per_device(): pl.pallas_call(functools.partial(kernel, (frames, height, cw, c0, c1, c2,...  30.9 us
    unnamed x1, local copies, waits for them, and re-layouts  1.35 us
    reshape x1, local copies, waits for them, and re-layouts, per_device(): gain_one.reshape(1, c1)  1.24 us
    reshape x1, local copies, waits for them, and re-layouts, per_device(): gain_two.reshape(1, c1)  1.24 us

profile of v1, /device:TPU:0, one launch (start us, length us, event | category | flops | bytes accessed | tf_op | source)
XLA Modules:
  0.0 34.7 jit_solution(2501750971697638537)
XLA Ops:
  0.0 1.2 %reshape.12.g1_ref = f32[1,384]{1,0:T(1,128)} reshape(f32[384]{0:T(512)} %param.12) | data formatting | bytes 3072 | tf_op jit(solution)/shard_map/reshape | solution.py:492
  1.2 1.2 %reshape.13.g2_ref = f32[1,384]{1,0:T(1,128)} reshape(f32[384]{0:T(512)} %param.14) | data formatting | bytes 3072 | tf_op jit(solution)/shard_map/reshape | solution.py:492
  2.5 30.9 %shard_map.100 = f32[4,3,2,256]{3,2,1,0:T(2,128)} custom-call(bf16[4,16,8,16]{3,2,1,0:T(8,128)(2,1)} %lat_hbm.1, f32[1,384]{1,0:T(1,128)} %reshape.12.g1_ref, f32[1,384]{1,0:T(1,128)} %reshape.13.g2_ref, f32[1,192]{1,0:T(1,128)} %bitcast.6, f32[1,96]{1,0:T(1,128)} %bitcast.7, bf16[3,3,3,16,384]{4,3,2,1,0:T(8,128)(2,1)} %win_hbm.1, ...), custom_call_target="tpu_custom_call" | custom-call | tf_op jit(solution)/shard_map/pallas_call | solution.py:453
  33.4 1.3 %copy.12 = f32[4,3,2,256]{3,2,1,0:T(2,128)} copy(f32[4,3,2,256]{3,2,1,0:T(2,128)} %shard_map.100) | data formatting | bytes 49152

commit v2 on v1

--- a/solution.py
+++ b/solution.py
@@ -50,13 +50,13 @@
 
 def kernel(
     sizes, devices, packed,
-    lat_hbm, g1_ref, g2_ref, g3_ref, g4_ref,
+    lat_hbm, g1_hbm, g2_hbm, g3_hbm, g4_hbm,
     win_hbm, wmid_hbm, wup_hbm, wlow_hbm, wout_hbm,
     out_ref,
-    raw_lat, lat_t, raw_in, raw_up, raw_low, raw_out,
+    g1_ref, g2_ref, g3_ref, g4_ref, raw_lat, lat_t, raw_in, raw_up, raw_low, raw_out,
     win, wmid, wupt, wup, wlow, wout_rows, wo, spread, g3x, g4x,
     latx, xs, first, a1, b1, b0, a3, act4, part, got, got_rows,
-    wsem, lsend, lrecv, hsend, hrecv, psend, precv,
+    wsem, known, lsend, lrecv, hsend, hrecv, psend, precv,
 ):
     frames, height, cw, c0, c1, c2, c3, colours = sizes
     ext = cw + 2
@@ -77,6 +77,9 @@
     load("lat", lat_hbm, latx.at[pl.ds(2, cw)] if packed else raw_lat, 0)
     load("in", win_hbm, raw_in, 1)
     load("out", wout_hbm, raw_out, 2)
+    gain_refs = [(g1_hbm, g1_ref), (g2_hbm, g2_ref), (g3_hbm, g3_ref), (g4_hbm, g4_ref)]
+    for i, (src, dst) in enumerate(gain_refs):
+        load(("gain", i), src, dst, 14 + i)
     load("up", wup_hbm, raw_up, 3)
     load("low", wlow_hbm, raw_low, 4)
     for a in range(3):
@@ -85,11 +88,26 @@
 
     barrier = pltpu.get_barrier_semaphore()
 
-    def greet(k, _):
-        pl.semaphore_signal(barrier, inc=1, device_id={"row": lax.rem(me + k, devices)}, device_id_type=MESH)
-        return _
-
-    lax.fori_loop(1, devices, greet, 0)
+    for peer, there in ((me - 1, has_left), (me + 1, has_right)):
+        @pl.when(there)
+        def _(peer=peer):
+            pl.semaphore_signal(barrier, inc=1, device_id={"row": peer}, device_id_type=MESH)
+
+    def tell(level):
+        step = 2**level
+        for side, peer in ((0, me - step), (1, me + step)):
+            @pl.when((peer >= 0) & (peer < devices))
+            def _(side=side, peer=peer):
+                pl.semaphore_signal(known.at[side, level], inc=1, device_id={"row": peer}, device_id_type=MESH)
+
+    def hear(level):
+        step = 2**level
+        for side, peer in ((1, me - step), (0, me + step)):
+            @pl.when((peer >= 0) & (peer < devices))
+            def _(side=side):
+                pl.semaphore_wait(known.at[side, level], 1)
+
+    levels = known.shape[1]
 
     copies["lat"].wait()
     if not packed:
@@ -104,7 +122,7 @@
         for j in range(cw):
             latx[2 + j] = lat_t[pl.ds(j, height, stride=cw), :].astype(bf16)
 
-    pl.semaphore_wait(barrier, devices - 1)
+    pl.semaphore_wait(barrier, has_left.astype(i32) + has_right.astype(i32))
 
     def lat_copy(right):
         peer = me + 1 if right else me - 1
@@ -122,6 +140,8 @@
     @pl.when(has_left)
     def _():
         lat_copy(False).start()
+
+    tell(0)
 
     @pl.when(is_first)
     def _():
@@ -147,7 +167,14 @@
                     win[at : at + c0, t * c1 : (t + 1) * c1] = block
         win[e * kx + 3 * fc : (e + 1) * kx, :] = jnp.zeros((kx - 3 * fc, frames * c1), bf16)
 
-    hg1, hg2 = g1_ref[...] * 0.5, g2_ref[...] * 0.5
+    for i in range(4):
+        copies[("gain", i)].wait()
+
+    def gain(ref):
+        rows = ref[...] * 0.5
+        return jnp.concatenate([rows[i : i + 1] for i in range(rows.shape[0])], axis=-1)
+
+    hg1, hg2 = gain(g1_ref), gain(g2_ref)
     g3x[0:1, 0:c2] = g3_ref[...] * 0.5
     g3x[0:1, c2 : 2 * c2] = g3_ref[...] * 0.5
     g4x[...] = jnp.zeros(g4x.shape, f32)
@@ -218,6 +245,9 @@
     for k in range(kinds):
         spread[:, k * full : (k + 1) * full] = (spot == k * nc + 1 + col).astype(bf16)
 
+    if 1 < levels:
+        hear(0)
+        tell(1)
     @pl.when(has_left)
     def _():
         lat_copy(True).wait_recv()
@@ -250,6 +280,9 @@
         a1[t, :, :, c1 : 2 * c1] = act.astype(bf16)
         a1[t, :, :, 2 * c1 : 3 * c1] = down.astype(bf16)
 
+    if 2 < levels:
+        hear(1)
+        tell(2)
     for a in range(3):
         for b in range(3):
             copies[("mid", a, b)].wait()
@@ -269,7 +302,12 @@
         s0, n = group_of[0], len(group_of)
         least = max(0, 3 - (frames - s0))
         lhs = jnp.concatenate([merge(a1[s0 : s0 + n, e : e + cw]) for e in range(3)], axis=-1)
-        d = dot(lhs, merge(wmid[:, :, :, least * c1 : 3 * c1]))
+        rhs = merge(wmid[:, :, :, least * c1 : 3 * c1])
+        paired = rhs.shape[1] // 512 * 512
+        cut = rhs.shape[0] // 512 * 256 + (256 if rhs.shape[0] % 512 else 0)
+        d = dot(lhs[:, :cut], rhs[:cut, paired:]) + dot(lhs[:, cut:], rhs[cut:, paired:])
+        if paired:
+            d = jnp.concatenate([dot(lhs, rhs[:, :paired]), d], axis=-1)
         for i, s in enumerate(group_of):
             for a in range(least, 3):
                 t = s - a + 2
@@ -326,6 +364,11 @@
     h2 = iota((height, 1), 0)
     even_kind = iota((1, LANES), 1) < colours * nc
 
+    for level in range(3, levels):
+        hear(level - 1)
+        tell(level)
+    hear(levels - 1)
+
     def message(t):
         def copy(k, act):
             peer = lax.rem(me + k, devices)
@@ -336,25 +379,32 @@
         return copy
 
     def lower(t):
-        total = None
+        half = wide // 2 * height
+        for i in range(2):
+            total = None
+            for a in range(3):
+                s = t + a - 2
+                if s < 0:
+                    continue
+                field = a3[s].reshape(nc, height, 4 * c2)
+                c = i * wide // 2
+                lhs = jnp.concatenate([merge(field[c + e : c + e + wide // 2]) for e in range(3)], axis=-1)
+                d = dot(lhs, wlow[a])
+                total = d if total is None else total + d
+            for q in range(2):
+                span = slice(q * LANES, (q + 1) * LANES)
+                act4[t, i * half : (i + 1) * half, span] = rms_act(total[:, span], hg4, c3).astype(bf16)
+        main, rest = None, [None, None]
         for a in range(3):
             s = t + a - 2
             if s < 0:
                 continue
-            field = a3[s].reshape(nc, height, 4 * c2)
-            lhs = jnp.concatenate([merge(field[e : e + wide]) for e in range(3)], axis=-1)
-            d = dot(lhs, wlow[a])
-            total = d if total is None else total + d
-        for q in range(2):
-            span = slice(q * LANES, (q + 1) * LANES)
-            act4[t, :, span] = rms_act(total[:, span], hg4, c3).astype(bf16)
-        total = None
-        for a in range(3):
-            s = t + a - 2
-            if s < 0:
-                continue
-            d = dot(act4[s], wo[a])
-            total = d if total is None else total + d
+            d = dot(act4[s], wo[a, :, : 4 * LANES])
+            main = d if main is None else main + d
+            for i in range(2):
+                d = dot(act4[s, i * half : (i + 1) * half], wo[a, :, 4 * LANES :])
+                rest[i] = d if rest[i] is None else rest[i] + d
+        total = jnp.concatenate([main, jnp.concatenate(rest, axis=0)], axis=-1)
         out = [None, None]
         for e in range(3):
             for c in range(wide):
@@ -409,6 +459,8 @@
     upsample(frames - 1)
     lower(frames - 1)
     for t in range(frames):
+        if t == frames - 1:
+            pass
         finish(t)
 
     @pl.when(has_right)
@@ -436,6 +488,7 @@
     ext, wide = cw + 2, 2 * cw
     full = wide * devices
     kinds = 2 * colours
+    levels = max(1, (devices - 1).bit_length())
     assert 2 * frames * c0 == LANES and kinds * (wide + 2) <= LANES
     packed = cw % 8 != 0
     if packed:
@@ -448,14 +501,18 @@
     tap_rows = -(-9 * colours // 16) * 16
 
     vmem = pl.BlockSpec(memory_space=pltpu.VMEM)
-    hbm = pl.BlockSpec(memory_space=pl.ANY)
+    hbm = pl.BlockSpec(memory_space=pltpu.HBM)
     dma = pltpu.SemaphoreType.DMA
     return pl.pallas_call(
         functools.partial(kernel, (frames, height, cw, c0, c1, c2, c3, colours), devices, packed),
         out_shape=jax.ShapeDtypeStruct((frames, colours, 2, full), f32),
-        in_specs=[hbm] + [vmem] * 4 + [hbm] * 5,
+        in_specs=[hbm] * 10,
         out_specs=vmem,
         scratch_shapes=[
+            pltpu.VMEM((c1 // LANES, LANES), f32),
+            pltpu.VMEM((c1 // LANES, LANES), f32),
+            pltpu.VMEM((1, c2), f32),
+            pltpu.VMEM((1, c3), f32),
             pltpu.VMEM(latent.shape, bf16),
             pltpu.VMEM((height * cw, LANES), f32),
             pltpu.VMEM(w_in.shape, bf16),
@@ -483,13 +540,13 @@
             pltpu.VMEM((frames, devices, 1, LANES), f32),
             pltpu.VMEM((frames, devices, 1, LANES), f32),
             pltpu.VMEM((devices, LANES), f32),
-            dma((14,)), dma((2,)), dma((2,)), dma((2, frames)), dma((2, frames)), dma((frames,)), dma((frames,)),
+            dma((18,)), pltpu.SemaphoreType.REGULAR((2, levels)), dma((2,)), dma((2,)), dma((2, frames)), dma((2, frames)), dma((frames,)), dma((frames,)),
         ],
         compiler_params=pltpu.CompilerParams(
-            collective_id=0, has_side_effects=True, vmem_limit_bytes=60 * 1024 * 1024
+            collective_id=0, has_side_effects=True, vmem_limit_bytes=57 * 1024 * 1024
         ),
     )(
-        lat, gain_one.reshape(1, c1), gain_two.reshape(1, c1), gain_three.reshape(1, c2), gain_four.reshape(1, c3),
+        lat, gain_one.reshape(-1, LANES), gain_two.reshape(-1, LANES), gain_three.reshape(1, c2), gain_four.reshape(1, c3),
         w_in, w_mid, wup, w_low, wout,
     )
 

time: 34.9 us -> 28.3 us (0.81)
  Pallas kernels: 30.9 us -> 26.8 us
  local copies, waits for them, and re-layouts: 3.84 us -> 1.35 us
    pallas_call x1, Pallas kernels: 30.9 us -> 26.8 us  [per_device(): pl.pallas_call(functools.partial(kernel, (frames, height, cw, c0, c1, c2,...]
    reshape x2 -> x0, local copies, waits for them, and re-layouts: 2.49 us -> none  [the longest x1 1.24 us: per_device(): gain_one.reshape(1, c1)]
where the time goes in v2:
time: 28.3 us; the launch traced here: 28.2 us
  Pallas kernels  26.8 us (95%)
  local copies, waits for them, and re-layouts  1.35 us (5%)
    pallas_call x1, Pallas kernels, per_device(): pl.pallas_call(functools.partial(kernel, (frames, height, cw, c0, c1, c2,...  26.8 us
    unnamed x1, local copies, waits for them, and re-layouts  1.35 us

profile of v2, /device:TPU:0, one launch (start us, length us, event | category | flops | bytes accessed | tf_op | source)
XLA Modules:
  0.0 28.2 jit_solution(10364620687650626219)
XLA Ops:
  0.0 26.8 %shard_map.100 = f32[4,3,2,256]{3,2,1,0:T(2,128)} custom-call(bf16[4,16,8,16]{3,2,1,0:T(8,128)(2,1)} %lat_hbm.1, f32[3,128]{1,0:T(4,128)} %bitcast.8, f32[3,128]{1,0:T(4,128)} %bitcast.9, f32[1,192]{1,0:T(1,128)} %bitcast.10, f32[1,96]{1,0:T(1,128)} %bitcast.11, bf16[3,3,3,16,384]{4,3,2,1,0:T(8,128)(2,1)} %win_hbm.1, bf16[3,3,3,384,384]{4,3,2,1,0:T(8,128)(2,1)} %wmid_hbm.1, ...), custom_call_target="tpu_custom_call" | custom-call | tf_op jit(solution)/shard_map/pallas_call | solution.py:506
  26.8 1.3 %copy.12 = f32[4,3,2,256]{3,2,1,0:T(2,128)} copy(f32[4,3,2,256]{3,2,1,0:T(2,128)} %shard_map.100) | data formatting | bytes 49152

commit v3 on v2

--- a/solution.py
+++ b/solution.py
@@ -76,15 +76,15 @@
 
     load("lat", lat_hbm, latx.at[pl.ds(2, cw)] if packed else raw_lat, 0)
     load("in", win_hbm, raw_in, 1)
-    load("out", wout_hbm, raw_out, 2)
     gain_refs = [(g1_hbm, g1_ref), (g2_hbm, g2_ref), (g3_hbm, g3_ref), (g4_hbm, g4_ref)]
     for i, (src, dst) in enumerate(gain_refs):
         load(("gain", i), src, dst, 14 + i)
-    load("up", wup_hbm, raw_up, 3)
+    load("out", wout_hbm, raw_out, 2)
     load("low", wlow_hbm, raw_low, 4)
     for a in range(3):
         for b in range(3):
             load(("mid", a, b), wmid_hbm.at[a, b], wmid.at[:, b, :, pl.ds(a * c1, c1)], 5 + 3 * a + b)
+    load("up", wup_hbm, raw_up, 3)
 
     barrier = pltpu.get_barrier_semaphore()
 
@@ -179,30 +179,6 @@
     g3x[0:1, c2 : 2 * c2] = g3_ref[...] * 0.5
     g4x[...] = jnp.zeros(g4x.shape, f32)
     g4x[0:1, 0:c3] = g4_ref[...] * 0.5
-
-    copies["up"].wait()
-    for row_odd in range(2):
-        for in_row in range(2):
-            mixed = []
-            for e in range(3):
-                if row_odd == 0:
-                    taps = (0, 1) if in_row == 0 else (2,)
-                else:
-                    taps = (0,) if in_row == 0 else (1, 2)
-                value = raw_up[taps[0], e].astype(f32)
-                for b in taps[1:]:
-                    value = value + raw_up[b, e].astype(f32)
-                mixed.append(value)
-            k0, k1, k2 = mixed
-            for parity in range(2):
-                pair = (k0 + k1, k2) if parity == 0 else (k0, k1 + k2)
-                at = parity * 2 * c2 + row_odd * c2
-                for in_col in range(2):
-                    wupt[in_row, at : at + c2, in_col * c1 : (in_col + 1) * c1] = pair[in_col].astype(bf16)
-    for in_row in range(2):
-        for i in range(0, 4 * c2, LANES):
-            for j in range(0, 2 * c1, LANES):
-                wup[in_row, j : j + LANES, i : i + LANES] = wupt[in_row, i : i + LANES, j : j + LANES].T
 
     copies["low"].wait()
     for a in range(3):
@@ -248,41 +224,64 @@
     if 1 < levels:
         hear(0)
         tell(1)
-    @pl.when(has_left)
-    def _():
-        lat_copy(True).wait_recv()
-
-    @pl.when(has_right)
-    def _():
-        lat_copy(False).wait_recv()
 
     h3 = iota((1, height, 1), 1)
     top3, bottom3 = h3 == 0, h3 == height - 1
     low_lanes = iota((1, 1, LANES), 2) < fc
-    for j in range(0, cw + 4, 2):
-        v = latx[j : j + 2].astype(f32)
-        up = jnp.where(top3, 0.0, pltpu.roll(v, 1, 1))
-        down = jnp.where(bottom3, 0.0, pltpu.roll(v, height - 1, 1))
-        xs[j : j + 2, :, 0:LANES] = jnp.where(low_lanes, up, v).astype(bf16)
-        xs[j : j + 2, :, LANES:kx] = jnp.where(low_lanes, down, 0.0).astype(bf16)
-
-    lhs = jnp.concatenate([merge(xs[e : e + ext]) for e in range(3)], axis=-1)
     keep_left, keep_right = has_left.astype(f32), has_right.astype(f32)
-    col_id = iota((ext * height, 1), 0)
-    keep = jnp.where(col_id < height, keep_left, jnp.where(col_id >= (ext - 1) * height, keep_right, 1.0))
-    for t in range(frames):
-        total = dot(lhs, win[:, t * c1 : (t + 1) * c1])
-        first[t] = total[height : (cw + 1) * height]
-        act = rows_of(rms_act(total, hg1, c1) * keep, ext)
-        up = jnp.where(top3, 0.0, pltpu.roll(act, 1, 1))
-        down = jnp.where(bottom3, 0.0, pltpu.roll(act, height - 1, 1))
-        a1[t, :, :, 0:c1] = up.astype(bf16)
-        a1[t, :, :, c1 : 2 * c1] = act.astype(bf16)
-        a1[t, :, :, 2 * c1 : 3 * c1] = down.astype(bf16)
+
+    def shift_rows(value):
+        up = jnp.where(top3, 0.0, pltpu.roll(value, 1, 1))
+        down = jnp.where(bottom3, 0.0, pltpu.roll(value, height - 1, 1))
+        return up, down
+
+    def stack_rows(j, n):
+        v = latx[j : j + n].astype(f32)
+        up, down = shift_rows(v)
+        xs[j : j + n, :, 0:LANES] = jnp.where(low_lanes, up, v).astype(bf16)
+        xs[j : j + n, :, LANES:kx] = jnp.where(low_lanes, down, 0.0).astype(bf16)
+
+    def first_conv(spans, keep):
+        lhs = jnp.concatenate(
+            [merge(jnp.concatenate([xs[j + e : j + e + n] for j, n in spans], axis=0)) for e in range(3)], axis=-1
+        )
+        for t in range(frames):
+            total = dot(lhs, win[:, t * c1 : (t + 1) * c1])
+            act = rms_act(total, hg1, c1)
+            if keep is not None:
+                act = act * keep
+            act = rows_of(act, act.shape[0] // height)
+            up, down = shift_rows(act)
+            at = 0
+            for j, n in spans:
+                for c in range(max(j, 1), min(j + n, cw + 1)):
+                    first[t, (c - 1) * height : c * height] = total[(at + c - j) * height : (at + c - j + 1) * height]
+                for k, value in enumerate((up, act, down)):
+                    a1[t, j : j + n, :, k * c1 : (k + 1) * c1] = value[at : at + n].astype(bf16)
+                at += n
+
+    stack_rows(2, cw)
+    if cw > 2:
+        first_conv([(2, cw - 2)], None)
+
+    @pl.when(has_left)
+    def _():
+        lat_copy(True).wait_recv()
+
+    @pl.when(has_right)
+    def _():
+        lat_copy(False).wait_recv()
+
+    stack_rows(0, 2)
+    stack_rows(cw + 2, 2)
+    place = iota((4 * height, 1), 0)
+    keep = jnp.where(place < height, keep_left, jnp.where(place >= 3 * height, keep_right, 1.0))
+    first_conv([(0, 2), (ext - 2, 2)], keep)
 
     if 2 < levels:
         hear(1)
         tell(2)
+
     for a in range(3):
         for b in range(3):
             copies[("mid", a, b)].wait()
@@ -295,36 +294,84 @@
             device_id={"row": peer}, device_id_type=MESH,
         )
 
+    def mix_up():
+        for row_odd in range(2):
+            for in_row in range(2):
+                mixed = []
+                for e in range(3):
+                    if row_odd == 0:
+                        taps = (0, 1) if in_row == 0 else (2,)
+                    else:
+                        taps = (0,) if in_row == 0 else (1, 2)
+                    value = raw_up[taps[0], e].astype(f32)
+                    for b in taps[1:]:
+                        value = value + raw_up[b, e].astype(f32)
+                    mixed.append(value)
+                k0, k1, k2 = mixed
+                for parity in range(2):
+                    pair = (k0 + k1, k2) if parity == 0 else (k0, k1 + k2)
+                    at = parity * 2 * c2 + row_odd * c2
+                    for in_col in range(2):
+                        wupt[in_row, at : at + c2, in_col * c1 : (in_col + 1) * c1] = pair[in_col].astype(bf16)
+        for in_row in range(2):
+            for i in range(0, 4 * c2, LANES):
+                for j in range(0, 2 * c1, LANES):
+                    wup[in_row, j : j + LANES, i : i + LANES] = wupt[in_row, i : i + LANES, j : j + LANES].T
+
+    copies["up"].wait()
     sums = {t: [] for t in range(frames)}
-    groups = [list(range(frames - 2)), [frames - 2], [frames - 1]]
     m = cw * height
-    for group_of in groups:
-        s0, n = group_of[0], len(group_of)
-        least = max(0, 3 - (frames - s0))
-        lhs = jnp.concatenate([merge(a1[s0 : s0 + n, e : e + cw]) for e in range(3)], axis=-1)
-        rhs = merge(wmid[:, :, :, least * c1 : 3 * c1])
+    tasks = [(0, 1, 2), (1, 2, 2), (0, 0, 0), (1, 0, 1)]
+    tasks = [(s, low, high) for s, low, high in tasks if s - high + 2 < frames]
+    tasks += [(s, max(0, 3 - frames + s), 2) for s in range(2, frames)]
+    assert frames >= 3
+    left = {t: min(3, t + 1) for t in range(frames)}
+    sent_count = 0
+    for s, least, most in tasks:
+        least = max(least, 3 - frames + s)
+        lhs = jnp.concatenate([merge(a1[s, e : e + cw]) for e in range(3)], axis=-1)
+        rhs = merge(wmid[:, :, :, least * c1 : (most + 1) * c1])
         paired = rhs.shape[1] // 512 * 512
         cut = rhs.shape[0] // 512 * 256 + (256 if rhs.shape[0] % 512 else 0)
         d = dot(lhs[:, :cut], rhs[:cut, paired:]) + dot(lhs[:, cut:], rhs[cut:, paired:])
         if paired:
             d = jnp.concatenate([dot(lhs, rhs[:, :paired]), d], axis=-1)
-        for i, s in enumerate(group_of):
-            for a in range(least, 3):
-                t = s - a + 2
-                sums[t].append(d[i * m : (i + 1) * m, (a - least) * c1 : (a - least + 1) * c1])
-        for t in group_of:
+        done = []
+        for a in range(least, most + 1):
+            t = s - a + 2
+            sums[t].append(d[:, (a - least) * c1 : (a - least + 1) * c1])
+            left[t] -= 1
+            if left[t] == 0:
+                done.append(t)
+        for t in done:
             total = first[t]
             for v in sums[t]:
                 total = total + v
             b1[t, 1 : cw + 1] = rows_of(rms_act(total, hg2, c1).astype(bf16), cw)
+            sent_count += 1
+
+        if done and sent_count > 1:
+            times = list(range(2)) if sent_count == 2 else done
 
             @pl.when(has_right)
-            def _(t=t):
-                halo(t, True).start()
+            def _(times=times):
+                for t in times:
+                    halo(t, True).start()
 
             @pl.when(has_left)
-            def _(t=t):
-                halo(t, False).start()
+            def _(times=times):
+                for t in times:
+                    halo(t, False).start()
+
+            if levels > 3 and sent_count == 2:
+                hear(2)
+                tell(3)
+            if sent_count == 2:
+                mix_up()
+            if sent_count == frames:
+                for level in range(4, levels):
+                    hear(level - 1)
+                    tell(level)
 
     low3 = iota((1, 2 * c2), 1) < c2
     pairs = cw + 1
@@ -333,15 +380,18 @@
     bottom = tall % height == height - 1
     hg3, hg4 = g3x[...], g4x[...]
 
-    def upsample(t):
+    def arrive(times):
         @pl.when(has_left)
         def _():
-            halo(t, True).wait_recv()
+            for t in times:
+                halo(t, True).wait_recv()
 
         @pl.when(has_right)
         def _():
-            halo(t, False).wait_recv()
-
+            for t in times:
+                halo(t, False).wait_recv()
+
+    def upsample(t):
         b0[t] = pltpu.roll(b1[t].astype(f32), 1, 1).astype(bf16)
         above = jnp.concatenate([merge(b0[t, e : e + pairs]) for e in range(2)], axis=-1)
         here = jnp.concatenate([merge(b1[t, e : e + pairs]) for e in range(2)], axis=-1)
@@ -363,11 +413,6 @@
     lane_mod = iota((1, LANES), 1) % nc
     h2 = iota((height, 1), 0)
     even_kind = iota((1, LANES), 1) < colours * nc
-
-    for level in range(3, levels):
-        hear(level - 1)
-        tell(level)
-    hear(levels - 1)
 
     def message(t):
         def copy(k, act):
@@ -419,8 +464,10 @@
             part[t, d] = value[d : d + 1]
         got[t, me] = part[t, me]
 
+    def send_all(times):
         def send(k, _):
-            message(t)(k, None).start()
+            for t in times:
+                message(t)(k, None).start()
             return _
 
         lax.fori_loop(1, devices, send, 0)
@@ -452,12 +499,22 @@
             row = jnp.sum(jnp.where(cell == source, d[:, k * full : (k + 1) * full], 0.0), axis=0, keepdims=True)
             out_ref[t, k % colours, k // colours : k // colours + 1, :] = row
 
-    for t in range(frames - 1):
-        upsample(t)
-    for t in range(frames - 1):
-        lower(t)
-    upsample(frames - 1)
-    lower(frames - 1)
+    blocks = [list(range(frames - 2)), [frames - 2], [frames - 1]]
+    for i, times in enumerate(blocks):
+        if i == 1:
+            pass
+        if i == 2:
+            pass
+        arrive(times)
+        if i == 1:
+            hear(levels - 1)
+        if i:
+            send_all(blocks[i - 1])
+        for t in times:
+            upsample(t)
+        for t in times:
+            lower(t)
+    send_all(blocks[-1])
     for t in range(frames):
         if t == frames - 1:
             pass
@@ -505,7 +562,7 @@
     dma = pltpu.SemaphoreType.DMA
     return pl.pallas_call(
         functools.partial(kernel, (frames, height, cw, c0, c1, c2, c3, colours), devices, packed),
-        out_shape=jax.ShapeDtypeStruct((frames, colours, 2, full), f32),
+        out_shape=pltpu.VMEM((frames, colours, 2, full), f32),
         in_specs=[hbm] * 10,
         out_specs=vmem,
         scratch_shapes=[

time: 28.3 us -> 25.1 us (0.89)
  Pallas kernels: 26.8 us -> 24.3 us
  local copies, waits for them, and re-layouts: 1.35 us -> 0.61 us
    pallas_call x1, Pallas kernels: 26.8 us -> 24.3 us  [per_device(): pl.pallas_call(functools.partial(kernel, (frames, height, cw, c0, c1, c2,...]
    unnamed x1, local copies, waits for them, and re-layouts: 1.35 us -> 0.61 us
where the time goes in v3:
time: 25.1 us; the launch traced here: 24.9 us
  Pallas kernels  24.3 us (97%)
  local copies, waits for them, and re-layouts  0.61 us (2%)
    pallas_call x1, Pallas kernels, per_device(): pl.pallas_call(functools.partial(kernel, (frames, height, cw, c0, c1, c2,...  24.3 us
    unnamed x1, local copies, waits for them, and re-layouts  0.61 us

profile of v3, /device:TPU:0, one launch (start us, length us, event | category | flops | bytes accessed | tf_op | source)
XLA Modules:
  0.0 24.9 jit_solution(2140038325323889576)
XLA Ops:
  0.0 24.3 %shard_map.100 = f32[4,3,2,256]{3,2,1,0:T(2,128)S(1)} custom-call(bf16[4,16,8,16]{3,2,1,0:T(8,128)(2,1)} %lat_hbm.1, f32[3,128]{1,0:T(4,128)} %bitcast.8, f32[3,128]{1,0:T(4,128)} %bitcast.9, f32[1,192]{1,0:T(1,128)} %bitcast.10, f32[1,96]{1,0:T(1,128)} %bitcast.11, bf16[3,3,3,16,384]{4,3,2,1,0:T(8,128)(2,1)} %win_hbm.1, ...), custom_call_target="tpu_custom_call" | custom-call | tf_op jit(solution)/shard_map/pallas_call | solution.py:563
  24.3 0.6 %copy.12 = f32[4,3,2,256]{3,2,1,0:T(2,128)} copy(f32[4,3,2,256]{3,2,1,0:T(2,128)S(1)} %shard_map.100) | data formatting | bytes 49152
